TPU v7x, 8 devices: a whole 2x2x1 slice. The times are simulated.
8 devices in a mesh: rep: 1 (over z), pp: 8 (over x, y, core).
Axes of the slice: x: 2, y: 2, z: 1, core: 2. Of those that a mesh axis runs over, the one named last changes fastest.
Arguments:
- x: bfloat16 [16, 512, 512], P('rep')
- dy: bfloat16 [16, 512, 512], P('rep')
- w_gate: bfloat16 [8, 512, 1408], P('pp')
- w_up: bfloat16 [8, 512, 1408], P('pp')
- w_down: bfloat16 [8, 1408, 512], P('pp')
Outputs:
- output 1: bfloat16 [8, 512, 1408], P(('rep', 'pp'))
- output 2: bfloat16 [8, 512, 1408], P(('rep', 'pp'))
- output 3: bfloat16 [8, 1408, 512], P(('rep', 'pp'))
All inputs are finite; a program needn't handle non-finite values.
Results may differ from a plain program's by a relative error of at most 0.0253.
Values are sent between devices in bfloat16 or wider.
A program may use at most 2 GiB of HBM per device.

v0:
```python
import jax
import jax.numpy as jnp
from jax import lax
from jax.sharding import PartitionSpec as P

NAMES = ("w_gate", "w_up", "w_down")


def matmul(a, w):
    return jnp.dot(a, w, preferred_element_type=jnp.float32).astype(jnp.bfloat16)


def normed(h):
    wide = h.astype(jnp.float32)
    scale = lax.rsqrt(jnp.mean(wide**2, -1, keepdims=True) + 1e-6)
    return (wide * scale).astype(jnp.bfloat16)


def layer(h, w):
    a = normed(h)
    gate = jnp.dot(a, w["w_gate"], preferred_element_type=jnp.float32)
    up = jnp.dot(a, w["w_up"], preferred_element_type=jnp.float32)
    return h + matmul((jax.nn.silu(gate) * up).astype(jnp.bfloat16), w["w_down"])


def stage(weights, h):
    for number in range(weights["w_gate"].shape[0]):
        h = layer(h, {name: w[number] for name, w in weights.items()})
    return h


def solution(mesh):
    stages = mesh.shape["pp"]
    onward = [(i, i + 1) for i in range(stages - 1)]
    back_again = [(i + 1, i) for i in range(stages - 1)]

    def step(x, dy, *arrays):
        weights = dict(zip(NAMES, arrays, strict=True))
        micro, me = x.shape[0], lax.axis_index("pp")
        kept, came = jnp.zeros_like(x), jnp.zeros_like(x[0])
        for t in range(micro + stages - 1):
            number = jnp.clip(t - me, 0, micro - 1)
            at_work = (t >= me) & (t - me < micro)
            h = jnp.where(me == 0, x[min(t, micro - 1)], came)
            was = lax.dynamic_index_in_dim(kept, number, 0, keepdims=False)
            kept = lax.dynamic_update_index_in_dim(kept, jnp.where(at_work, h, was), number, 0)
            came = lax.ppermute(stage(weights, h), "pp", onward)
        total = {name: jnp.zeros(w.shape, jnp.float32) for name, w in weights.items()}
        came, behind = jnp.zeros_like(x[0]), stages - 1 - me
        for t in range(micro + stages - 1):
            number = jnp.clip(t - behind, 0, micro - 1)
            at_work = (t >= behind) & (t - behind < micro)
            by_y = jnp.where(behind == 0, dy[min(t, micro - 1)], came)
            _, back = jax.vjp(stage, weights, lax.dynamic_index_in_dim(kept, number, 0, keepdims=False))
            by_w, by_h = back(by_y)
            total = {name: total[name] + jnp.where(at_work, by_w[name].astype(jnp.float32), 0.0) for name in NAMES}
            came = lax.ppermute(by_h, "pp", back_again)
        return tuple(total[name].astype(jnp.bfloat16) for name in NAMES)

    return jax.shard_map(
        step,
        mesh=mesh,
        in_specs=(P("rep", None, None),) * 2 + (P("pp", None, None),) * 3,
        out_specs=(P(("rep", "pp"), None, None),) * 3,
        check_vma=False,
    )
```

profile of v0, /device:TPU:5, one launch (start us, length us, event | category | flops | bytes accessed | tf_op | source)
XLA Modules:
  0.0 1065.8 jit_solution(9195996258423224348)
XLA Ops:
  5.9 5.2 fusion.1037
  14.7 6.1 collective-permute-done
  24.8 5.3 fusion.1034
  30.1 5.3 collective-permute-start.1
  35.4 6.1 collective-permute-done.1
  45.4 5.3 fusion.1031
  50.8 5.3 collective-permute-start.2
  56.1 6.1 collective-permute-done.2
  66.9 5.6 fusion.1028
  72.4 5.8 collective-permute-start.3
  78.2 5.6 collective-permute-done.3
  88.5 5.6 fusion.1025
  94.1 5.3 collective-permute-start.4
  99.4 6.1 collective-permute-done.4
  110.2 5.6 fusion.1022
  115.8 5.3 collective-permute-start.5
  121.1 6.1 collective-permute-done.5
  131.9 5.6 fusion.1019
  137.5 5.3 collective-permute-start.6
  142.8 6.1 collective-permute-done.6
  153.6 5.6 fusion.1016
  159.2 5.5 collective-permute-start.7
  164.7 5.9 collective-permute-done.7
  175.3 5.6 fusion.1013
  180.9 5.3 collective-permute-start.8
  186.2 6.1 collective-permute-done.8
  197.0 5.6 fusion.1010
  202.6 5.3 collective-permute-start.9
  208.0 6.0 collective-permute-done.9
  218.9 5.2 fusion.1007
  224.1 5.4 collective-permute-start.10
  243.5 5.2 fusion.1004
  261.9 5.2 fusion.1001
  267.2 5.4 collective-permute-start.12
  283.5 5.3 fusion.998
  288.7 5.4 collective-permute-start.13
  305.0 5.3 fusion.995
  310.3 5.4 collective-permute-start.14
  326.6 5.2 fusion.992
  331.9 5.8 collective-permute-start.15
  348.4 5.3 fusion.989
  353.6 5.2 collective-permute-start.16
  369.7 5.3 fusion.986
  375.0 5.4 collective-permute-start.17
  391.3 5.3 fusion.983
  396.5 5.4 collective-permute-start.18
  412.8 5.2 fusion.980
  418.1 5.6 collective-permute-start.19
  434.4 5.2 fusion.977
  439.6 5.4 collective-permute-start.20
  455.9 5.3 fusion.974
  461.2 5.4 collective-permute-start.21
  498.0 5.1 collective-permute-done.22
  543.5 5.0 collective-permute-done.24
  568.8 5.0 collective-permute-done.25
  644.7 5.0 collective-permute-done.28
  670.0 5.0 collective-permute-done.29
  745.9 5.0 collective-permute-done.32
  771.2 5.0 collective-permute-done.33
  847.1 5.0 collective-permute-done.36
  872.5 5.0 collective-permute-done.37
  948.4 5.0 collective-permute-done.40
  973.7 5.0 collective-permute-done.41
  1040.7 24.6 %fusion.305 = bf16[1,1408,512]{2,1,0:T(8,128)(2,1)} fusion(f32[1408,512]{1,0:T(8,128)} %fusion.68, f32[1408,512]{1,0:T(8,128)} %fusion.66, f32[1408,512]{1,0:T(8,128)} %fusion.64, f32[1408,512]{1,0:T(8,128)} %fusion.62, f32[1408,512]{1,0:T(8,128)} %fusion.60, f32[1408,512]{1,0:T(8,128)} %fusion.58, f32[1408,512]{1,0:T(8,128)} %fusion.56, ...), kind=kOutput, calls=%fused_computation.531 | convolution fusion | flops 761266176 | bytes 71172096 | tf_op jit(solution)/shard_map/transpose(jvp())/dot_general | solution.py:10
  (530 shorter events, 695.7 us)
Async XLA Ops:
  11.1 9.7 collective-permute-start
  30.1 11.4 %collective-permute-start.1 = (bf16[512,512]{1,0:T(8,128)(2,1)}, bf16[512,512]{1,0:T(8,128)(2,1)S(1)}, u32[]{:S(2)}, u32[]{:S(2)}) collective-permute-start(bf16[512,512]{1,0:T(8,128)(2,1)} %fusion.1034), channel_id=1, source_target_pairs={{0,1},{1,2},{2,3},{3,4},{4,5},{5,6},{6,7}} | collective-permute-start | bytes 1572872 | tf_op jit(solution)/shard_map/ppermute | solution.py:47
  50.8 11.4 %collective-permute-start.2 = (bf16[512,512]{1,0:T(8,128)(2,1)}, bf16[512,512]{1,0:T(8,128)(2,1)S(1)}, u32[]{:S(2)}, u32[]{:S(2)}) collective-permute-start(bf16[512,512]{1,0:T(8,128)(2,1)} %fusion.1031), channel_id=1, source_target_pairs={{0,1},{1,2},{2,3},{3,4},{4,5},{5,6},{6,7}} | collective-permute-start | bytes 1572872 | tf_op jit(solution)/shard_map/ppermute | solution.py:47
  72.4 11.4 %collective-permute-start.3 = (bf16[512,512]{1,0:T(8,128)(2,1)}, bf16[512,512]{1,0:T(8,128)(2,1)S(1)}, u32[]{:S(2)}, u32[]{:S(2)}) collective-permute-start(bf16[512,512]{1,0:T(8,128)(2,1)} %fusion.1028), channel_id=1, source_target_pairs={{0,1},{1,2},{2,3},{3,4},{4,5},{5,6},{6,7}} | collective-permute-start | bytes 1572872 | tf_op jit(solution)/shard_map/ppermute | solution.py:47
  94.1 11.4 %collective-permute-start.4 = (bf16[512,512]{1,0:T(8,128)(2,1)}, bf16[512,512]{1,0:T(8,128)(2,1)S(1)}, u32[]{:S(2)}, u32[]{:S(2)}) collective-permute-start(bf16[512,512]{1,0:T(8,128)(2,1)} %fusion.1025), channel_id=1, source_target_pairs={{0,1},{1,2},{2,3},{3,4},{4,5},{5,6},{6,7}} | collective-permute-start | bytes 1572872 | tf_op jit(solution)/shard_map/ppermute | solution.py:47
  115.8 11.4 %collective-permute-start.5 = (bf16[512,512]{1,0:T(8,128)(2,1)}, bf16[512,512]{1,0:T(8,128)(2,1)S(1)}, u32[]{:S(2)}, u32[]{:S(2)}) collective-permute-start(bf16[512,512]{1,0:T(8,128)(2,1)} %fusion.1022), channel_id=1, source_target_pairs={{0,1},{1,2},{2,3},{3,4},{4,5},{5,6},{6,7}} | collective-permute-start | bytes 1572872 | tf_op jit(solution)/shard_map/ppermute | solution.py:47
  137.5 11.4 %collective-permute-start.6 = (bf16[512,512]{1,0:T(8,128)(2,1)}, bf16[512,512]{1,0:T(8,128)(2,1)S(1)}, u32[]{:S(2)}, u32[]{:S(2)}) collective-permute-start(bf16[512,512]{1,0:T(8,128)(2,1)} %fusion.1019), channel_id=1, source_target_pairs={{0,1},{1,2},{2,3},{3,4},{4,5},{5,6},{6,7}} | collective-permute-start | bytes 1572872 | tf_op jit(solution)/shard_map/ppermute | solution.py:47
  159.2 11.4 %collective-permute-start.7 = (bf16[512,512]{1,0:T(8,128)(2,1)}, bf16[512,512]{1,0:T(8,128)(2,1)S(1)}, u32[]{:S(2)}, u32[]{:S(2)}) collective-permute-start(bf16[512,512]{1,0:T(8,128)(2,1)} %fusion.1016), channel_id=1, source_target_pairs={{0,1},{1,2},{2,3},{3,4},{4,5},{5,6},{6,7}} | collective-permute-start | bytes 1572872 | tf_op jit(solution)/shard_map/ppermute | solution.py:47
  180.9 11.4 %collective-permute-start.8 = (bf16[512,512]{1,0:T(8,128)(2,1)}, bf16[512,512]{1,0:T(8,128)(2,1)S(1)}, u32[]{:S(2)}, u32[]{:S(2)}) collective-permute-start(bf16[512,512]{1,0:T(8,128)(2,1)} %fusion.1013), channel_id=1, source_target_pairs={{0,1},{1,2},{2,3},{3,4},{4,5},{5,6},{6,7}} | collective-permute-start | bytes 1572872 | tf_op jit(solution)/shard_map/ppermute | solution.py:47
  202.6 11.4 %collective-permute-start.9 = (bf16[512,512]{1,0:T(8,128)(2,1)}, bf16[512,512]{1,0:T(8,128)(2,1)}, u32[]{:S(2)}, u32[]{:S(2)}) collective-permute-start(bf16[512,512]{1,0:T(8,128)(2,1)} %fusion.1010), channel_id=1, source_target_pairs={{0,1},{1,2},{2,3},{3,4},{4,5},{5,6},{6,7}} | collective-permute-start | bytes 1572872 | tf_op jit(solution)/shard_map/ppermute | solution.py:47
  224.1 11.4 %copy-start.45 = (bf16[1,1408,512]{2,1,0:T(8,128)(2,1)S(1)}, bf16[1,1408,512]{2,1,0:T(8,128)(2,1)}, u32[]{:S(2)}) copy-start(bf16[1,1408,512]{2,1,0:T(8,128)(2,1)} %param.9) | copy-start | bytes 4325380
  224.1 14.6 %collective-permute-start.10 = (bf16[512,512]{1,0:T(8,128)(2,1)}, bf16[512,512]{1,0:T(8,128)(2,1)S(1)}, u32[]{:S(2)}, u32[]{:S(2)}) collective-permute-start(bf16[512,512]{1,0:T(8,128)(2,1)} %fusion.1007), channel_id=1, source_target_pairs={{0,1},{1,2},{2,3},{3,4},{4,5},{5,6},{6,7}} | collective-permute-start | bytes 1572872 | tf_op jit(solution)/shard_map/ppermute | solution.py:47
  248.7 8.3 collective-permute-start.11
  267.2 8.5 copy-start.9
  267.2 11.5 %collective-permute-start.12 = (bf16[512,512]{1,0:T(8,128)(2,1)}, bf16[512,512]{1,0:T(8,128)(2,1)S(1)}, u32[]{:S(2)}, u32[]{:S(2)}) collective-permute-start(bf16[512,512]{1,0:T(8,128)(2,1)} %fusion.1001), channel_id=1, source_target_pairs={{0,1},{1,2},{2,3},{3,4},{4,5},{5,6},{6,7}} | collective-permute-start | bytes 1572872 | tf_op jit(solution)/shard_map/ppermute | solution.py:47
  283.5 10.7 %copy-start.4 = (bf16[512,512]{1,0:T(8,128)(2,1)S(1)}, bf16[512,512]{1,0:T(8,128)(2,1)}, u32[]{:S(2)}) copy-start(bf16[512,512]{1,0:T(8,128)(2,1)} %copy-done.3) | copy-start | bytes 1572868
  288.7 8.5 copy-start.13
  288.7 11.5 %collective-permute-start.13 = (bf16[512,512]{1,0:T(8,128)(2,1)}, bf16[512,512]{1,0:T(8,128)(2,1)S(1)}, u32[]{:S(2)}, u32[]{:S(2)}) collective-permute-start(bf16[512,512]{1,0:T(8,128)(2,1)} %fusion.998), channel_id=1, source_target_pairs={{0,1},{1,2},{2,3},{3,4},{4,5},{5,6},{6,7}} | collective-permute-start | bytes 1572872 | tf_op jit(solution)/shard_map/ppermute | solution.py:47
  305.0 10.7 %copy-start.7 = (bf16[512,512]{1,0:T(8,128)(2,1)S(1)}, bf16[512,512]{1,0:T(8,128)(2,1)}, u32[]{:S(2)}) copy-start(bf16[512,512]{1,0:T(8,128)(2,1)} %copy-done.6) | copy-start | bytes 1572868
  310.3 8.5 copy-start.15
  310.3 11.5 %collective-permute-start.14 = (bf16[512,512]{1,0:T(8,128)(2,1)}, bf16[512,512]{1,0:T(8,128)(2,1)S(1)}, u32[]{:S(2)}, u32[]{:S(2)}) collective-permute-start(bf16[512,512]{1,0:T(8,128)(2,1)} %fusion.995), channel_id=1, source_target_pairs={{0,1},{1,2},{2,3},{3,4},{4,5},{5,6},{6,7}} | collective-permute-start | bytes 1572872 | tf_op jit(solution)/shard_map/ppermute | solution.py:47
  326.6 11.1 %copy-start.11 = (bf16[512,512]{1,0:T(8,128)(2,1)S(1)}, bf16[512,512]{1,0:T(8,128)(2,1)}, u32[]{:S(2)}) copy-start(bf16[512,512]{1,0:T(8,128)(2,1)} %copy-done.10) | copy-start | bytes 1572868
  331.9 8.9 copy-start.17
  331.9 11.7 %collective-permute-start.15 = (bf16[512,512]{1,0:T(8,128)(2,1)}, bf16[512,512]{1,0:T(8,128)(2,1)S(1)}, u32[]{:S(2)}, u32[]{:S(2)}) collective-permute-start(bf16[512,512]{1,0:T(8,128)(2,1)} %fusion.992), channel_id=1, source_target_pairs={{0,1},{1,2},{2,3},{3,4},{4,5},{5,6},{6,7}} | collective-permute-start | bytes 1572872 | tf_op jit(solution)/shard_map/ppermute | solution.py:47
  348.4 10.5 copy-start.19
  353.6 11.3 %collective-permute-start.16 = (bf16[512,512]{1,0:T(8,128)(2,1)}, bf16[512,512]{1,0:T(8,128)(2,1)S(1)}, u32[]{:S(2)}, u32[]{:S(2)}) collective-permute-start(bf16[512,512]{1,0:T(8,128)(2,1)} %fusion.989), channel_id=1, source_target_pairs={{0,1},{1,2},{2,3},{3,4},{4,5},{5,6},{6,7}} | collective-permute-start | bytes 1572872 | tf_op jit(solution)/shard_map/ppermute | solution.py:47
  369.7 10.7 %copy-start.23 = (bf16[512,512]{1,0:T(8,128)(2,1)S(1)}, bf16[512,512]{1,0:T(8,128)(2,1)}, u32[]{:S(2)}) copy-start(bf16[512,512]{1,0:T(8,128)(2,1)} %copy-done.22) | copy-start | bytes 1572868
  375.0 8.5 copy-start.25
  375.0 11.5 %collective-permute-start.17 = (bf16[512,512]{1,0:T(8,128)(2,1)}, bf16[512,512]{1,0:T(8,128)(2,1)S(1)}, u32[]{:S(2)}, u32[]{:S(2)}) collective-permute-start(bf16[512,512]{1,0:T(8,128)(2,1)} %fusion.986), channel_id=1, source_target_pairs={{0,1},{1,2},{2,3},{3,4},{4,5},{5,6},{6,7}} | collective-permute-start | bytes 1572872 | tf_op jit(solution)/shard_map/ppermute | solution.py:47
  391.3 10.7 %copy-start.27 = (bf16[512,512]{1,0:T(8,128)(2,1)S(1)}, bf16[512,512]{1,0:T(8,128)(2,1)}, u32[]{:S(2)}) copy-start(bf16[512,512]{1,0:T(8,128)(2,1)} %copy-done.26) | copy-start | bytes 1572868
  396.5 8.5 copy-start.29
  396.5 11.5 %collective-permute-start.18 = (bf16[512,512]{1,0:T(8,128)(2,1)}, bf16[512,512]{1,0:T(8,128)(2,1)S(1)}, u32[]{:S(2)}, u32[]{:S(2)}) collective-permute-start(bf16[512,512]{1,0:T(8,128)(2,1)} %fusion.983), channel_id=1, source_target_pairs={{0,1},{1,2},{2,3},{3,4},{4,5},{5,6},{6,7}} | collective-permute-start | bytes 1572872 | tf_op jit(solution)/shard_map/ppermute | solution.py:47
  412.8 10.9 %copy-start.31 = (bf16[512,512]{1,0:T(8,128)(2,1)S(1)}, bf16[512,512]{1,0:T(8,128)(2,1)}, u32[]{:S(2)}) copy-start(bf16[512,512]{1,0:T(8,128)(2,1)} %copy-done.30) | copy-start | bytes 1572868
  418.1 8.7 copy-start.33
  418.1 11.5 %collective-permute-start.19 = (bf16[512,512]{1,0:T(8,128)(2,1)}, bf16[512,512]{1,0:T(8,128)(2,1)S(1)}, u32[]{:S(2)}, u32[]{:S(2)}) collective-permute-start(bf16[512,512]{1,0:T(8,128)(2,1)} %fusion.980), channel_id=1, source_target_pairs={{0,1},{1,2},{2,3},{3,4},{4,5},{5,6},{6,7}} | collective-permute-start | bytes 1572872 | tf_op jit(solution)/shard_map/ppermute | solution.py:47
  434.4 10.7 %copy-start.35 = (bf16[512,512]{1,0:T(8,128)(2,1)S(1)}, bf16[512,512]{1,0:T(8,128)(2,1)}, u32[]{:S(2)}) copy-start(bf16[512,512]{1,0:T(8,128)(2,1)} %copy-done.34) | copy-start | bytes 1572868
  439.6 8.5 copy-start.37
  439.6 11.5 %collective-permute-start.20 = (bf16[512,512]{1,0:T(8,128)(2,1)}, bf16[512,512]{1,0:T(8,128)(2,1)S(1)}, u32[]{:S(2)}, u32[]{:S(2)}) collective-permute-start(bf16[512,512]{1,0:T(8,128)(2,1)} %fusion.977), channel_id=1, source_target_pairs={{0,1},{1,2},{2,3},{3,4},{4,5},{5,6},{6,7}} | collective-permute-start | bytes 1572872 | tf_op jit(solution)/shard_map/ppermute | solution.py:47
  455.9 10.7 %copy-start.39 = (bf16[512,512]{1,0:T(8,128)(2,1)S(1)}, bf16[512,512]{1,0:T(8,128)(2,1)}, u32[]{:S(2)}) copy-start(bf16[512,512]{1,0:T(8,128)(2,1)} %copy-done.38) | copy-start | bytes 1572868
  461.2 8.5 copy-start.41
  461.2 11.5 %collective-permute-start.21 = (bf16[512,512]{1,0:T(8,128)(2,1)}, bf16[512,512]{1,0:T(8,128)(2,1)S(1)}, u32[]{:S(2)}, u32[]{:S(2)}) collective-permute-start(bf16[512,512]{1,0:T(8,128)(2,1)} %fusion.974), channel_id=1, source_target_pairs={{0,1},{1,2},{2,3},{3,4},{4,5},{5,6},{6,7}} | collective-permute-start | bytes 1572872 | tf_op jit(solution)/shard_map/ppermute | solution.py:47
  490.9 12.2 %collective-permute-start.22 = (bf16[512,512]{1,0:T(8,128)(2,1)S(1)}, bf16[512,512]{1,0:T(8,128)(2,1)S(1)}, u32[]{:S(2)}, u32[]{:S(2)}) collective-permute-start(bf16[512,512]{1,0:T(8,128)(2,1)S(1)} %fusion.1306), channel_id=1, source_target_pairs={{1,0},{2,1},{3,2},{4,3},{5,4},{6,5},{7,6}} | collective-permute-start | bytes 1572872 | tf_op jit(solution)/shard_map/ppermute | solution.py:57
  495.2 9.1 copy-start.2
  511.9 11.4 %collective-permute-start.23 = (bf16[512,512]{1,0:T(8,128)(2,1)S(1)}, bf16[512,512]{1,0:T(8,128)(2,1)S(1)}, u32[]{:S(2)}, u32[]{:S(2)}) collective-permute-start(bf16[512,512]{1,0:T(8,128)(2,1)S(1)} %fusion.1305), channel_id=1, source_target_pairs={{1,0},{2,1},{3,2},{4,3},{5,4},{6,5},{7,6}} | collective-permute-start | bytes 1572872 | tf_op jit(solution)/shard_map/ppermute | solution.py:57
  537.1 11.4 %collective-permute-start.24 = (bf16[512,512]{1,0:T(8,128)(2,1)S(1)}, bf16[512,512]{1,0:T(8,128)(2,1)S(1)}, u32[]{:S(2)}, u32[]{:S(2)}) collective-permute-start(bf16[512,512]{1,0:T(8,128)(2,1)S(1)} %fusion.1304), channel_id=1, source_target_pairs={{1,0},{2,1},{3,2},{4,3},{5,4},{6,5},{7,6}} | collective-permute-start | bytes 1572872 | tf_op jit(solution)/shard_map/ppermute | solution.py:57
  562.4 11.4 %collective-permute-start.25 = (bf16[512,512]{1,0:T(8,128)(2,1)S(1)}, bf16[512,512]{1,0:T(8,128)(2,1)S(1)}, u32[]{:S(2)}, u32[]{:S(2)}) collective-permute-start(bf16[512,512]{1,0:T(8,128)(2,1)S(1)} %fusion.1303), channel_id=1, source_target_pairs={{1,0},{2,1},{3,2},{4,3},{5,4},{6,5},{7,6}} | collective-permute-start | bytes 1572872 | tf_op jit(solution)/shard_map/ppermute | solution.py:57
  587.7 11.4 %collective-permute-start.26 = (bf16[512,512]{1,0:T(8,128)(2,1)S(1)}, bf16[512,512]{1,0:T(8,128)(2,1)S(1)}, u32[]{:S(2)}, u32[]{:S(2)}) collective-permute-start(bf16[512,512]{1,0:T(8,128)(2,1)S(1)} %fusion.1302), channel_id=1, source_target_pairs={{1,0},{2,1},{3,2},{4,3},{5,4},{6,5},{7,6}} | collective-permute-start | bytes 1572872 | tf_op jit(solution)/shard_map/ppermute | solution.py:57
  613.0 11.4 %collective-permute-start.27 = (bf16[512,512]{1,0:T(8,128)(2,1)S(1)}, bf16[512,512]{1,0:T(8,128)(2,1)S(1)}, u32[]{:S(2)}, u32[]{:S(2)}) collective-permute-start(bf16[512,512]{1,0:T(8,128)(2,1)S(1)} %fusion.1301), channel_id=1, source_target_pairs={{1,0},{2,1},{3,2},{4,3},{5,4},{6,5},{7,6}} | collective-permute-start | bytes 1572872 | tf_op jit(solution)/shard_map/ppermute | solution.py:57
  638.3 11.4 %collective-permute-start.28 = (bf16[512,512]{1,0:T(8,128)(2,1)S(1)}, bf16[512,512]{1,0:T(8,128)(2,1)S(1)}, u32[]{:S(2)}, u32[]{:S(2)}) collective-permute-start(bf16[512,512]{1,0:T(8,128)(2,1)S(1)} %fusion.1300), channel_id=1, source_target_pairs={{1,0},{2,1},{3,2},{4,3},{5,4},{6,5},{7,6}} | collective-permute-start | bytes 1572872 | tf_op jit(solution)/shard_map/ppermute | solution.py:57
  663.6 11.4 %collective-permute-start.29 = (bf16[512,512]{1,0:T(8,128)(2,1)S(1)}, bf16[512,512]{1,0:T(8,128)(2,1)S(1)}, u32[]{:S(2)}, u32[]{:S(2)}) collective-permute-start(bf16[512,512]{1,0:T(8,128)(2,1)S(1)} %fusion.1299), channel_id=1, source_target_pairs={{1,0},{2,1},{3,2},{4,3},{5,4},{6,5},{7,6}} | collective-permute-start | bytes 1572872 | tf_op jit(solution)/shard_map/ppermute | solution.py:57
  688.9 11.4 %collective-permute-start.30 = (bf16[512,512]{1,0:T(8,128)(2,1)S(1)}, bf16[512,512]{1,0:T(8,128)(2,1)S(1)}, u32[]{:S(2)}, u32[]{:S(2)}) collective-permute-start(bf16[512,512]{1,0:T(8,128)(2,1)S(1)} %fusion.1298), channel_id=1, source_target_pairs={{1,0},{2,1},{3,2},{4,3},{5,4},{6,5},{7,6}} | collective-permute-start | bytes 1572872 | tf_op jit(solution)/shard_map/ppermute | solution.py:57
  714.2 11.4 %collective-permute-start.31 = (bf16[512,512]{1,0:T(8,128)(2,1)S(1)}, bf16[512,512]{1,0:T(8,128)(2,1)S(1)}, u32[]{:S(2)}, u32[]{:S(2)}) collective-permute-start(bf16[512,512]{1,0:T(8,128)(2,1)S(1)} %fusion.1297), channel_id=1, source_target_pairs={{1,0},{2,1},{3,2},{4,3},{5,4},{6,5},{7,6}} | collective-permute-start | bytes 1572872 | tf_op jit(solution)/shard_map/ppermute | solution.py:57
  739.5 11.4 %collective-permute-start.32 = (bf16[512,512]{1,0:T(8,128)(2,1)S(1)}, bf16[512,512]{1,0:T(8,128)(2,1)S(1)}, u32[]{:S(2)}, u32[]{:S(2)}) collective-permute-start(bf16[512,512]{1,0:T(8,128)(2,1)S(1)} %fusion.1296), channel_id=1, source_target_pairs={{1,0},{2,1},{3,2},{4,3},{5,4},{6,5},{7,6}} | collective-permute-start | bytes 1572872 | tf_op jit(solution)/shard_map/ppermute | solution.py:57
  764.8 11.4 %collective-permute-start.33 = (bf16[512,512]{1,0:T(8,128)(2,1)S(1)}, bf16[512,512]{1,0:T(8,128)(2,1)S(1)}, u32[]{:S(2)}, u32[]{:S(2)}) collective-permute-start(bf16[512,512]{1,0:T(8,128)(2,1)S(1)} %fusion.1295), channel_id=1, source_target_pairs={{1,0},{2,1},{3,2},{4,3},{5,4},{6,5},{7,6}} | collective-permute-start | bytes 1572872 | tf_op jit(solution)/shard_map/ppermute | solution.py:57
  790.1 11.4 %collective-permute-start.34 = (bf16[512,512]{1,0:T(8,128)(2,1)S(1)}, bf16[512,512]{1,0:T(8,128)(2,1)S(1)}, u32[]{:S(2)}, u32[]{:S(2)}) collective-permute-start(bf16[512,512]{1,0:T(8,128)(2,1)S(1)} %fusion.1294), channel_id=1, source_target_pairs={{1,0},{2,1},{3,2},{4,3},{5,4},{6,5},{7,6}} | collective-permute-start | bytes 1572872 | tf_op jit(solution)/shard_map/ppermute | solution.py:57
  815.4 11.4 %collective-permute-start.35 = (bf16[512,512]{1,0:T(8,128)(2,1)S(1)}, bf16[512,512]{1,0:T(8,128)(2,1)S(1)}, u32[]{:S(2)}, u32[]{:S(2)}) collective-permute-start(bf16[512,512]{1,0:T(8,128)(2,1)S(1)} %fusion.1293), channel_id=1, source_target_pairs={{1,0},{2,1},{3,2},{4,3},{5,4},{6,5},{7,6}} | collective-permute-start | bytes 1572872 | tf_op jit(solution)/shard_map/ppermute | solution.py:57
  840.8 11.4 %collective-permute-start.36 = (bf16[512,512]{1,0:T(8,128)(2,1)S(1)}, bf16[512,512]{1,0:T(8,128)(2,1)S(1)}, u32[]{:S(2)}, u32[]{:S(2)}) collective-permute-start(bf16[512,512]{1,0:T(8,128)(2,1)S(1)} %fusion.1292), channel_id=1, source_target_pairs={{1,0},{2,1},{3,2},{4,3},{5,4},{6,5},{7,6}} | collective-permute-start | bytes 1572872 | tf_op jit(solution)/shard_map/ppermute | solution.py:57
  866.1 11.4 %collective-permute-start.37 = (bf16[512,512]{1,0:T(8,128)(2,1)S(1)}, bf16[512,512]{1,0:T(8,128)(2,1)S(1)}, u32[]{:S(2)}, u32[]{:S(2)}) collective-permute-start(bf16[512,512]{1,0:T(8,128)(2,1)S(1)} %fusion.1291), channel_id=1, source_target_pairs={{1,0},{2,1},{3,2},{4,3},{5,4},{6,5},{7,6}} | collective-permute-start | bytes 1572872 | tf_op jit(solution)/shard_map/ppermute | solution.py:57
  891.4 11.4 %collective-permute-start.38 = (bf16[512,512]{1,0:T(8,128)(2,1)S(1)}, bf16[512,512]{1,0:T(8,128)(2,1)S(1)}, u32[]{:S(2)}, u32[]{:S(2)}) collective-permute-start(bf16[512,512]{1,0:T(8,128)(2,1)S(1)} %fusion.1290), channel_id=1, source_target_pairs={{1,0},{2,1},{3,2},{4,3},{5,4},{6,5},{7,6}} | collective-permute-start | bytes 1572872 | tf_op jit(solution)/shard_map/ppermute | solution.py:57
  916.8 11.4 %collective-permute-start.39 = (bf16[512,512]{1,0:T(8,128)(2,1)S(1)}, bf16[512,512]{1,0:T(8,128)(2,1)S(1)}, u32[]{:S(2)}, u32[]{:S(2)}) collective-permute-start(bf16[512,512]{1,0:T(8,128)(2,1)S(1)} %fusion.1289), channel_id=1, source_target_pairs={{1,0},{2,1},{3,2},{4,3},{5,4},{6,5},{7,6}} | collective-permute-start | bytes 1572872 | tf_op jit(solution)/shard_map/ppermute | solution.py:57
  942.1 11.4 %collective-permute-start.40 = (bf16[512,512]{1,0:T(8,128)(2,1)S(1)}, bf16[512,512]{1,0:T(8,128)(2,1)S(1)}, u32[]{:S(2)}, u32[]{:S(2)}) collective-permute-start(bf16[512,512]{1,0:T(8,128)(2,1)S(1)} %fusion.1288), channel_id=1, source_target_pairs={{1,0},{2,1},{3,2},{4,3},{5,4},{6,5},{7,6}} | collective-permute-start | bytes 1572872 | tf_op jit(solution)/shard_map/ppermute | solution.py:57
  967.3 11.4 %collective-permute-start.41 = (bf16[512,512]{1,0:T(8,128)(2,1)S(1)}, bf16[512,512]{1,0:T(8,128)(2,1)S(1)}, u32[]{:S(2)}, u32[]{:S(2)}) collective-permute-start(bf16[512,512]{1,0:T(8,128)(2,1)S(1)} %fusion.1287), channel_id=1, source_target_pairs={{1,0},{2,1},{3,2},{4,3},{5,4},{6,5},{7,6}} | collective-permute-start | bytes 1572872 | tf_op jit(solution)/shard_map/ppermute | solution.py:57
  992.7 11.4 %collective-permute-start.42 = (bf16[512,512]{1,0:T(8,128)(2,1)S(1)}, bf16[512,512]{1,0:T(8,128)(2,1)S(1)}, u32[]{:S(2)}, u32[]{:S(2)}) collective-permute-start(bf16[512,512]{1,0:T(8,128)(2,1)S(1)} %fusion.1286), channel_id=1, source_target_pairs={{1,0},{2,1},{3,2},{4,3},{5,4},{6,5},{7,6}} | collective-permute-start | bytes 1572872 | tf_op jit(solution)/shard_map/ppermute | solution.py:57
  1018.1 11.4 %collective-permute-start.43 = (bf16[512,512]{1,0:T(8,128)(2,1)S(1)}, bf16[512,512]{1,0:T(8,128)(2,1)S(1)}, u32[]{:S(2)}, u32[]{:S(2)}) collective-permute-start(bf16[512,512]{1,0:T(8,128)(2,1)S(1)} %fusion.1285), channel_id=1, source_target_pairs={{1,0},{2,1},{3,2},{4,3},{5,4},{6,5},{7,6}} | collective-permute-start | bytes 1572872 | tf_op jit(solution)/shard_map/ppermute | solution.py:57
  (30 other events, 73.6 us)
where the time goes:
time: 1080 us; the launch traced here: 1070 us
  matrix products  584 us (54%)
  waiting for transfers between devices  168 us (16%)
  starting transfers between devices  163 us (15%)
  other arithmetic  96.5 us (9%)
  local copies, waits for them, and re-layouts  50.8 us (5%)
    dot_general x68, matrix products, matmul(): jnp.dot(a, w, preferred_element_type=jnp.float32).astype(jnp.bfloat16)  228 us
    dot_general x90, matrix products, layer(): gate = jnp.dot(a, w['w_gate'], preferred_element_type=jnp.float32)  197 us
    dot_general x68, matrix products, layer(): up = jnp.dot(a, w['w_up'], preferred_element_type=jnp.float32)  159 us
    ppermute x22, starting transfers between devices, step(): came = lax.ppermute(stage(weights, h), 'pp', onward)  114 us
    ppermute x22, waiting for transfers between devices, step(): came = lax.ppermute(by_h, 'pp', back_again)  104 us
    ppermute x22, waiting for transfers between devices, step(): came = lax.ppermute(stage(weights, h), 'pp', onward)  64.2 us
    ppermute x22, starting transfers between devices, step(): came = lax.ppermute(by_h, 'pp', back_again)  48.2 us
    dynamic_update_slice x23, other arithmetic, step(): lax.dynamic_update_index_in_dim(kept, jnp.where(at_work, h, was), number, 0)  34.3 us
  transfers between devices with their start and end apart: 44, of which 41 were waited for; matrix products, arithmetic and copies ran while one was open for 16% of the time, Pallas kernels for 0%

commit v1 on v0

v1 whole, which is shorter than its diff:
```python
import jax
import jax.numpy as jnp
from jax import lax
from jax.experimental import pallas as pl
from jax.experimental.pallas import tpu as pltpu
from jax.sharding import PartitionSpec as P

F32, BF16 = jnp.float32, jnp.bfloat16
ROWS = 256
RING = 4
EPS = 1e-6
AHEAD = (16, 16, 16, 16, 16, 16, 16, 0)


def dot(a, b):
    return jnp.dot(a, b, preferred_element_type=F32)


def kernel(
    x, dy, w_gate, w_up, w_down, o_gate, o_up, o_down,
    f_in, b_in, f_out, b_out, w_both, w_d, wt_d, wt_g, wt_u, acc_both, acc_d, a_t, hid, hid_t, d_both,
    f_recv, b_recv, f_send, b_send, w_sem, o_sem,
):
    micro, tokens, d = x.shape
    ff = w_down.shape[0]
    parts = tokens // ROWS
    blocks = ff // 128
    me = lax.axis_index("pp")
    stages = 8
    first, last = me == 0, me == stages - 1

    def w_copies():
        for j in range(blocks):
            src = pl.ds(128 * j, 128)
            yield pltpu.make_async_copy(w_gate.at[:, src], w_both.at[:, pl.ds(256 * j, 128)], w_sem.at[0, j])
            yield pltpu.make_async_copy(w_up.at[:, src], w_both.at[:, pl.ds(256 * j + 128, 128)], w_sem.at[1, j])
        yield pltpu.make_async_copy(w_down, w_d, w_sem.at[0, blocks])

    def chunk(ref, c):
        return ref.at[c // parts, pl.ds(pl.multiple_of((c % parts) * ROWS, ROWS), ROWS)]

    def f_copy(c):
        return pltpu.make_async_remote_copy(
            f_out.at[c % RING], chunk(f_in, c), f_send.at[c % RING], f_recv.at[c], device_id={"pp": jnp.minimum(me + 1, stages - 1)}
        )

    def b_copy(c):
        return pltpu.make_async_remote_copy(
            b_out.at[c % RING], chunk(b_in, c), b_send.at[c % RING], b_recv.at[c], device_id={"pp": jnp.maximum(me - 1, 0)}
        )

    for copy in w_copies():
        copy.start()

    @pl.when(first)
    def _():
        @pl.loop(0, micro * parts)
        def _(c):
            pltpu.make_async_copy(chunk(x, c), chunk(f_in, c), f_recv.at[c]).start()

    @pl.when(last)
    def _():
        @pl.loop(0, micro * parts)
        def _(c):
            pltpu.make_async_copy(chunk(dy, c), chunk(b_in, c), b_recv.at[c]).start()

    barrier = pltpu.get_barrier_semaphore()
    for other in range(1, stages):
        pl.semaphore_signal(barrier, inc=1, device_id={"pp": lax.rem(me + other, stages)})
    acc_both[...] = jnp.zeros_like(acc_both)
    acc_d[...] = jnp.zeros_like(acc_d)
    pl.semaphore_wait(barrier, stages - 1)

    for copy in w_copies():
        copy.wait()

    def scale_of(wide):
        return lax.rsqrt(jnp.mean(wide * wide, -1, keepdims=True) + EPS)

    def forward(c):
        f_copy(c).wait_recv()
        h = chunk(f_in, c)[...]

        @pl.when(~last)
        def _():
            wide = h.astype(F32)
            a = (wide * scale_of(wide)).astype(BF16)
            for j in range(blocks):
                both = dot(a, w_both[:, 256 * j : 256 * j + 256])
                gate, up = both[:, :128], both[:, 128:]
                hid[:, 128 * j : 128 * j + 128] = (gate * jax.nn.sigmoid(gate) * up).astype(BF16)

            @pl.when(c >= RING)
            def _():
                f_copy(c - RING).wait_send()

            f_out[c % RING] = h + dot(hid[...], w_d[...]).astype(BF16)
            f_copy(c).start()

    def backward(c):
        b_copy(c).wait_recv()
        rows = pl.ds(pl.multiple_of((c % parts) * ROWS, ROWS), ROWS)
        by_y = chunk(b_in, c)[...]
        wide = chunk(f_in, c)[...].astype(F32)
        scale = scale_of(wide)
        a = (wide * scale).astype(BF16)
        a_t[:, rows] = a.T
        for j in range(0, blocks, 2):
            n = min(2, blocks - j)
            by_hid = dot(by_y, wt_d[:, 128 * j : 128 * (j + n)]).astype(BF16).astype(F32)
            for k in range(j, j + n):
                both = dot(a, w_both[:, 256 * k : 256 * k + 256])
                gate, up = both[:, :128], both[:, 128:]
                by = by_hid[:, 128 * (k - j) : 128 * (k - j) + 128]
                sig = jax.nn.sigmoid(gate)
                silu = gate * sig
                hid_t[128 * k : 128 * k + 128, rows] = (silu * up).astype(BF16).T
                d_both[rows, ff + 128 * k : ff + 128 * k + 128] = (by * silu).astype(BF16)
                by_silu = by * up
                d_both[rows, 128 * k : 128 * k + 128] = (by_silu * (sig + silu * (1 - sig))).astype(BF16)

        @pl.when(~first)
        def _():
            by_a = (dot(d_both[rows, :ff], wt_g[...]).astype(BF16) + dot(d_both[rows, ff:], wt_u[...]).astype(BF16)).astype(F32)
            wide = chunk(f_in, c)[...].astype(F32)
            scale = scale_of(wide)
            by_scale = jnp.sum(by_a * wide, -1, keepdims=True)
            by_wide = by_a * scale - wide * (by_scale * scale * scale * scale * (1.0 / d))

            @pl.when(c >= RING)
            def _():
                b_copy(c - RING).wait_send()

            b_out[c % RING] = chunk(b_in, c)[...] + by_wide.astype(BF16)
            b_copy(c).start()

    def by_weights(m):
        for j in range(2 * blocks // 2):
            cols = slice(256 * j, 256 * j + 256)
            acc_both[:, cols] += dot(a_t[...], d_both[:, cols]).astype(BF16).astype(F32)
        by_y = b_in[m]
        for j in range(0, ff, 352):
            rows = slice(j, j + 352)
            acc_d[rows, :] += dot(hid_t[rows, :], by_y).astype(BF16).astype(F32)

    ahead = jnp.int32(0)
    for s, k in enumerate(AHEAD):
        ahead = jnp.where(me == s, k, ahead)

    @pl.loop(0, micro + max(AHEAD))
    def _(i):
        @pl.when(i < micro)
        def _():
            @pl.loop(0, parts)
            def _(p):
                forward(parts * i + p)

        @pl.when(i == 0)
        def _():
            @pl.loop(0, blocks)
            def _(j):
                cols = pl.ds(pl.multiple_of(128 * j, 128), 128)
                wt_d[:, cols] = w_d[cols, :].T
                wt_g[cols, :] = w_both[:, pl.ds(pl.multiple_of(256 * j, 128), 128)].T
                wt_u[cols, :] = w_both[:, pl.ds(pl.multiple_of(256 * j + 128, 128), 128)].T

        m = i - ahead

        @pl.when((m >= 0) & (m < micro))
        def _():
            @pl.loop(0, parts)
            def _(p):
                backward(parts * m + p)

            by_weights(m)

    for c in range(micro * parts - RING, micro * parts):

        @pl.when(~last)
        def _():
            f_copy(c).wait_send()

        @pl.when(~first)
        def _():
            b_copy(c).wait_send()

    d_both[...] = acc_both[...].astype(BF16)
    hid_t[...] = acc_d[...].astype(BF16)
    out = (
        pltpu.make_async_copy(d_both.at[:, pl.ds(0, ff)], o_gate, o_sem.at[0]),
        pltpu.make_async_copy(d_both.at[:, pl.ds(ff, ff)], o_up, o_sem.at[1]),
        pltpu.make_async_copy(hid_t, o_down, o_sem.at[2]),
    )
    for copy in out:
        copy.start()
    for copy in out:
        copy.wait()


def solution(mesh):
    def step(x, dy, w_gate, w_up, w_down):
        micro, tokens, d = x.shape
        ff = w_down.shape[1]
        chunks = micro * tokens // ROWS
        hbm = pl.BlockSpec(memory_space=pl.ANY)
        dma = pltpu.SemaphoreType.DMA
        outs = pl.pallas_call(
            kernel,
            out_shape=tuple(jax.ShapeDtypeStruct(w.shape[1:], w.dtype) for w in (w_gate, w_up, w_down)),
            in_specs=[hbm] * 5,
            out_specs=(hbm,) * 3,
            scratch_shapes=[
                pltpu.VMEM((micro, tokens, d), BF16),
                pltpu.VMEM((micro, tokens, d), BF16),
                pltpu.VMEM((RING, ROWS, d), BF16),
                pltpu.VMEM((RING, ROWS, d), BF16),
                pltpu.VMEM((d, 2 * ff), BF16),
                pltpu.VMEM((ff, d), BF16),
                pltpu.VMEM((d, ff), BF16),
                pltpu.VMEM((ff, d), BF16),
                pltpu.VMEM((ff, d), BF16),
                pltpu.VMEM((d, 2 * ff), F32),
                pltpu.VMEM((ff, d), F32),
                pltpu.VMEM((d, tokens), BF16),
                pltpu.VMEM((ROWS, ff), BF16),
                pltpu.VMEM((ff, tokens), BF16),
                pltpu.VMEM((tokens, 2 * ff), BF16),
                dma((chunks,)),
                dma((chunks,)),
                dma((RING,)),
                dma((RING,)),
                dma((2, ff // 128 + 1)),
                dma((3,)),
            ],
            compiler_params=pltpu.CompilerParams(
                collective_id=0, has_side_effects=True, vmem_limit_bytes=60 * 1024 * 1024
            ),
        )(x, dy, w_gate[0], w_up[0], w_down[0])
        return tuple(o[None] for o in outs)

    return jax.shard_map(
        step,
        mesh=mesh,
        in_specs=(P("rep", None, None),) * 2 + (P("pp", None, None),) * 3,
        out_specs=(P(("rep", "pp"), None, None),) * 3,
        check_vma=False,
    )
```

time: 1080 us -> 289 us (0.27)
  the two profiles are of different devices: /device:TPU:5 before, /device:TPU:0 now
where the time goes in v1:
time: 289 us
  Pallas kernels  283 us (98%)
  local copies, waits for them, and re-layouts  5.66 us (2%)
    pallas_call x1, Pallas kernels, step(): pl.pallas_call(kernel, out_shape=tuple((jax.ShapeDtypeStruct(w.shape[1:],...  283 us

profile of v1, /device:TPU:0, one launch (start us, length us, event | category | flops | bytes accessed | tf_op | source)
XLA Modules:
  0.0 289.1 jit_solution(8451718133539558156)
XLA Ops:
  0.6 282.8 %shard_map.76 = (bf16[512,1408]{1,0:T(8,128)(2,1)}, bf16[512,1408]{1,0:T(8,128)(2,1)}, bf16[1408,512]{1,0:T(8,128)(2,1)}) custom-call(bf16[16,512,512]{2,1,0:T(8,128)(2,1)} %x.1, bf16[16,512,512]{2,1,0:T(8,128)(2,1)} %dy.1, bf16[512,1408]{1,0:T(8,128)(2,1)} %bitcast.9, bf16[512,1408]{1,0:T(8,128)(2,1)} %bitcast.10, bf16[1408,512]{1,0:T(8,128)(2,1)} %bitcast.11), custom_call_target="tpu_custom_call" | custom-call | tf_op jit(solution)/shard_map/pallas_call | solution.py:207
  283.5 0.0 copy-start.1
  283.5 2.7 copy.11
  286.1 0.0 copy-done.1
  286.2 0.0 copy-start
  286.2 1.1 copy.12
  287.3 0.8 copy-done
  288.0 1.1 copy.13
Async XLA Ops:
  283.5 2.7 copy-start.1
  286.2 1.9 copy-start

commit v2 on v1

--- a/solution.py
+++ b/solution.py
@@ -9,7 +9,7 @@
 ROWS = 256
 RING = 4
 EPS = 1e-6
-AHEAD = (16, 16, 16, 16, 16, 16, 16, 0)
+AHEAD = (14, 13, 11, 10, 6, 5, 2, 0)
 
 
 def dot(a, b):
@@ -17,9 +17,9 @@
 
 
 def kernel(
-    x, dy, w_gate, w_up, w_down, o_gate, o_up, o_down,
-    f_in, b_in, f_out, b_out, w_both, w_d, wt_d, wt_g, wt_u, acc_both, acc_d, a_t, hid, hid_t, d_both,
-    f_recv, b_recv, f_send, b_send, w_sem, o_sem,
+    x, dy, w_gate, w_up, w_down, o_gate, o_up, o_down, kept_pq, kept_hid,
+    f_in, b_in, f_out, b_out, w_both, w_d, wt_d, wt_g, wt_u, acc_both, acc_d, a_t, hid_t, d_both, pq_out, hid_out, pq_in, hid_in,
+    f_recv, b_recv, f_send, b_send, w_sem, o_sem, out_sem, in_sem,
 ):
     micro, tokens, d = x.shape
     ff = w_down.shape[0]
@@ -49,6 +49,20 @@
             b_out.at[c % RING], chunk(b_in, c), b_send.at[c % RING], b_recv.at[c], device_id={"pp": jnp.maximum(me - 1, 0)}
         )
 
+    def kept_out(c):
+        slot = c % 2
+        return (
+            pltpu.make_async_copy(pq_out.at[slot], kept_pq.at[c], out_sem.at[0, slot]),
+            pltpu.make_async_copy(hid_out.at[slot], kept_hid.at[c], out_sem.at[1, slot]),
+        )
+
+    def kept_in(c):
+        slot = c % 2
+        return (
+            pltpu.make_async_copy(kept_pq.at[c], pq_in.at[slot], in_sem.at[0, slot]),
+            pltpu.make_async_copy(kept_hid.at[c], hid_in.at[slot], in_sem.at[1, slot]),
+        )
+
     for copy in w_copies():
         copy.start()
 
@@ -77,62 +91,102 @@
     def scale_of(wide):
         return lax.rsqrt(jnp.mean(wide * wide, -1, keepdims=True) + EPS)
 
+    def gates(both):
+        gate, up = both[:, :128], both[:, 128:]
+        sig = jax.nn.sigmoid(gate)
+        silu = gate * sig
+        return silu, up * (sig + silu * (1 - sig)), (silu * up).astype(BF16)
+
     def forward(c):
         f_copy(c).wait_recv()
-        h = chunk(f_in, c)[...]
 
         @pl.when(~last)
         def _():
+            slot = c % 2
+
+            @pl.when(c >= 2)
+            def _():
+                for copy in kept_out(c - 2):
+                    copy.wait()
+
+            @pl.when(c >= RING)
+            def _():
+                f_copy(c - RING).wait_send()
+
+            h = chunk(f_in, c)[...]
             wide = h.astype(F32)
             a = (wide * scale_of(wide)).astype(BF16)
             for j in range(blocks):
-                both = dot(a, w_both[:, 256 * j : 256 * j + 256])
-                gate, up = both[:, :128], both[:, 128:]
-                hid[:, 128 * j : 128 * j + 128] = (gate * jax.nn.sigmoid(gate) * up).astype(BF16)
-
-            @pl.when(c >= RING)
-            def _():
-                f_copy(c - RING).wait_send()
-
-            f_out[c % RING] = h + dot(hid[...], w_d[...]).astype(BF16)
+                silu, by_gate, hid = gates(dot(a, w_both[:, 256 * j : 256 * j + 256]))
+                pq_out[slot, :, 256 * j : 256 * j + 128] = silu
+                pq_out[slot, :, 256 * j + 128 : 256 * j + 256] = by_gate
+                hid_out[slot, :, 128 * j : 128 * j + 128] = hid
+            f_out[c % RING] = h + dot(hid_out[slot], w_d[...]).astype(BF16)
             f_copy(c).start()
-
-    def backward(c):
+            for copy in kept_out(c):
+                copy.start()
+
+    def rows_of(c):
+        return pl.ds(pl.multiple_of((c % parts) * ROWS, ROWS), ROWS)
+
+    def backward_last(c):
         b_copy(c).wait_recv()
-        rows = pl.ds(pl.multiple_of((c % parts) * ROWS, ROWS), ROWS)
+        rows = rows_of(c)
         by_y = chunk(b_in, c)[...]
         wide = chunk(f_in, c)[...].astype(F32)
-        scale = scale_of(wide)
-        a = (wide * scale).astype(BF16)
+        a = (wide * scale_of(wide)).astype(BF16)
         a_t[:, rows] = a.T
         for j in range(0, blocks, 2):
             n = min(2, blocks - j)
             by_hid = dot(by_y, wt_d[:, 128 * j : 128 * (j + n)]).astype(BF16).astype(F32)
             for k in range(j, j + n):
-                both = dot(a, w_both[:, 256 * k : 256 * k + 256])
-                gate, up = both[:, :128], both[:, 128:]
+                silu, by_gate, hid = gates(dot(a, w_both[:, 256 * k : 256 * k + 256]))
                 by = by_hid[:, 128 * (k - j) : 128 * (k - j) + 128]
-                sig = jax.nn.sigmoid(gate)
-                silu = gate * sig
-                hid_t[128 * k : 128 * k + 128, rows] = (silu * up).astype(BF16).T
+                hid_t[128 * k : 128 * k + 128, rows] = hid.T
+                d_both[rows, 128 * k : 128 * k + 128] = (by * by_gate).astype(BF16)
                 d_both[rows, ff + 128 * k : ff + 128 * k + 128] = (by * silu).astype(BF16)
-                by_silu = by * up
-                d_both[rows, 128 * k : 128 * k + 128] = (by_silu * (sig + silu * (1 - sig))).astype(BF16)
+        send_back(c)
+
+    def backward(c):
+        @pl.when(c + 1 < micro * parts)
+        def _():
+            for copy in kept_in(c + 1):
+                copy.start()
+
+        for copy in kept_in(c):
+            copy.wait()
+        b_copy(c).wait_recv()
+        slot = c % 2
+        rows = rows_of(c)
+        by_y = chunk(b_in, c)[...]
+        wide = chunk(f_in, c)[...].astype(F32)
+        a_t[:, rows] = (wide * scale_of(wide)).astype(BF16).T
+        hid_t[:, rows] = hid_in[slot].T
+        for j in range(0, blocks, 2):
+            n = min(2, blocks - j)
+            by_hid = dot(by_y, wt_d[:, 128 * j : 128 * (j + n)]).astype(BF16).astype(F32)
+            for k in range(j, j + n):
+                by = by_hid[:, 128 * (k - j) : 128 * (k - j) + 128]
+                d_both[rows, 128 * k : 128 * k + 128] = (by * pq_in[slot, :, 256 * k + 128 : 256 * k + 256]).astype(BF16)
+                d_both[rows, ff + 128 * k : ff + 128 * k + 128] = (by * pq_in[slot, :, 256 * k : 256 * k + 128]).astype(BF16)
 
         @pl.when(~first)
         def _():
-            by_a = (dot(d_both[rows, :ff], wt_g[...]).astype(BF16) + dot(d_both[rows, ff:], wt_u[...]).astype(BF16)).astype(F32)
-            wide = chunk(f_in, c)[...].astype(F32)
-            scale = scale_of(wide)
-            by_scale = jnp.sum(by_a * wide, -1, keepdims=True)
-            by_wide = by_a * scale - wide * (by_scale * scale * scale * scale * (1.0 / d))
-
-            @pl.when(c >= RING)
-            def _():
-                b_copy(c - RING).wait_send()
-
-            b_out[c % RING] = chunk(b_in, c)[...] + by_wide.astype(BF16)
-            b_copy(c).start()
+            send_back(c)
+
+    def send_back(c):
+        @pl.when(c >= RING)
+        def _():
+            b_copy(c - RING).wait_send()
+
+        rows = rows_of(c)
+        wide = chunk(f_in, c)[...].astype(F32)
+        scale = scale_of(wide)
+        by_a = (dot(d_both[rows, :ff], wt_g[...]).astype(BF16) + dot(d_both[rows, ff:], wt_u[...]).astype(BF16)).astype(F32)
+        by_scale = jnp.sum(by_a * wide, -1, keepdims=True)
+        by_wide = by_a * scale - wide * (by_scale * scale * scale * scale * (1.0 / d))
+        b_out[c % RING] = chunk(b_in, c)[...] + by_wide.astype(BF16)
+        b_copy(c).start()
 
     def by_weights(m):
         for j in range(2 * blocks // 2):
@@ -164,13 +218,30 @@
                 wt_g[cols, :] = w_both[:, pl.ds(pl.multiple_of(256 * j, 128), 128)].T
                 wt_u[cols, :] = w_both[:, pl.ds(pl.multiple_of(256 * j + 128, 128), 128)].T
 
+        @pl.when((i == micro) & ~last)
+        def _():
+            for c in range(micro * parts - 2, micro * parts):
+                for copy in kept_out(c):
+                    copy.wait()
+
+        @pl.when((i == ahead - 1) & ~last)
+        def _():
+            for copy in kept_in(0):
+                copy.start()
+
         m = i - ahead
 
         @pl.when((m >= 0) & (m < micro))
         def _():
             @pl.loop(0, parts)
             def _(p):
-                backward(parts * m + p)
+                @pl.when(last)
+                def _():
+                    backward_last(parts * m + p)
+
+                @pl.when(~last)
+                def _():
+                    backward(parts * m + p)
 
             by_weights(m)
 
@@ -206,9 +277,13 @@
         dma = pltpu.SemaphoreType.DMA
         outs = pl.pallas_call(
             kernel,
-            out_shape=tuple(jax.ShapeDtypeStruct(w.shape[1:], w.dtype) for w in (w_gate, w_up, w_down)),
+            out_shape=(
+                *(jax.ShapeDtypeStruct(w.shape[1:], w.dtype) for w in (w_gate, w_up, w_down)),
+                jax.ShapeDtypeStruct((chunks, ROWS, 2 * ff), F32),
+                jax.ShapeDtypeStruct((chunks, ROWS, ff), BF16),
+            ),
             in_specs=[hbm] * 5,
-            out_specs=(hbm,) * 3,
+            out_specs=(hbm,) * 5,
             scratch_shapes=[
                 pltpu.VMEM((micro, tokens, d), BF16),
                 pltpu.VMEM((micro, tokens, d), BF16),
@@ -222,21 +297,26 @@
                 pltpu.VMEM((d, 2 * ff), F32),
                 pltpu.VMEM((ff, d), F32),
                 pltpu.VMEM((d, tokens), BF16),
-                pltpu.VMEM((ROWS, ff), BF16),
                 pltpu.VMEM((ff, tokens), BF16),
                 pltpu.VMEM((tokens, 2 * ff), BF16),
+                pltpu.VMEM((2, ROWS, 2 * ff), F32),
+                pltpu.VMEM((2, ROWS, ff), BF16),
+                pltpu.VMEM((2, ROWS, 2 * ff), F32),
+                pltpu.VMEM((2, ROWS, ff), BF16),
                 dma((chunks,)),
                 dma((chunks,)),
                 dma((RING,)),
                 dma((RING,)),
                 dma((2, ff // 128 + 1)),
                 dma((3,)),
+                dma((2, 2)),
+                dma((2, 2)),
             ],
             compiler_params=pltpu.CompilerParams(
-                collective_id=0, has_side_effects=True, vmem_limit_bytes=60 * 1024 * 1024
+                collective_id=0, has_side_effects=True, vmem_limit_bytes=67_043_328
             ),
         )(x, dy, w_gate[0], w_up[0], w_down[0])
-        return tuple(o[None] for o in outs)
+        return tuple(o[None] for o in outs[:3])
 
     return jax.shard_map(
         step,

time: 289 us -> 259 us (0.90)
  Pallas kernels: 283 us -> 253 us
    pallas_call x1, Pallas kernels: 283 us -> 253 us  [step(): pl.pallas_call(kernel, out_shape=(*(jax.ShapeDtypeStruct(w.shape[1:], w.d...]
where the time goes in v2:
time: 259 us
  Pallas kernels  253 us (98%)
  local copies, waits for them, and re-layouts  5.66 us (2%)
    pallas_call x1, Pallas kernels, step(): pl.pallas_call(kernel, out_shape=(*(jax.ShapeDtypeStruct(w.shape[1:], w.d...  253 us
    unnamed x7, local copies, waits for them, and re-layouts  5.66 us

profile of v2, /device:TPU:0, one launch (start us, length us, event | category | flops | bytes accessed | tf_op | source)
XLA Modules:
  0.0 259.0 jit_solution(6234061213841768996)
XLA Ops:
  0.6 252.7 %shard_map.76 = (bf16[512,1408]{1,0:T(8,128)(2,1)}, bf16[512,1408]{1,0:T(8,128)(2,1)}, bf16[1408,512]{1,0:T(8,128)(2,1)}, f32[32,256,2816]{2,1,0:T(8,128)}, bf16[32,256,1408]{2,1,0:T(8,128)(2,1)}) custom-call(bf16[16,512,512]{2,1,0:T(8,128)(2,1)} %x.1, bf16[16,512,512]{2,1,0:T(8,128)(2,1)} %dy.1, bf16[512,1408]{1,0:T(8,128)(2,1)} %bitcast.9, ...), custom_call_target="tpu_custom_call" | custom-call | tf_op jit(solution)/shard_map/pallas_call | solution.py:278
  253.3 0.0 copy-start.1
  253.3 2.7 %copy.11 = bf16[1,512,1408]{2,1,0:T(8,128)(2,1)} copy(bf16[1,512,1408]{2,1,0:T(8,128)(2,1)} %bitcast.8) | data formatting | bytes 2883584
  256.0 0.0 copy-done.1
  256.0 0.0 copy-start
  256.0 1.1 copy.12
  257.1 0.8 copy-done
  257.9 1.1 copy.13
Async XLA Ops:
  253.3 2.7 %copy-start.1 = (bf16[512,1408]{1,0:T(8,128)(2,1)S(1)}, bf16[512,1408]{1,0:T(8,128)(2,1)}, u32[]{:S(2)}) copy-start(bf16[512,1408]{1,0:T(8,128)(2,1)} %get-tuple-element.7) | copy-start | bytes 4325380
  256.0 1.9 copy-start

commit v3 on v1

v3 whole, which is shorter than its diff:
```python
import jax
import jax.numpy as jnp
from jax import lax
from jax.experimental import pallas as pl
from jax.experimental.pallas import tpu as pltpu
from jax.sharding import PartitionSpec as P

F32, BF16 = jnp.float32, jnp.bfloat16
EPS = 1e-6
Q = 128
COARSE, FINE = 256, 128
AHEAD = (14, 13, 10, 9, 6, 5, 2, 0)
FINE_F = 6
FINE_B = 6
FINE_E = 6
RELAY_F, RELAY_B = 0, 7
LAG_F = 3
LAG_B = 3


def dot(a, b):
    return jnp.dot(a, b, preferred_element_type=F32)


def kernel(
    x, dy, w_gate, w_up, w_down, o_gate, o_up, o_down, kept_pq, kept_hid,
    f_in, b_in, r_in, f_out, b_out, w_both, w_d, wt_d, wt_g, wt_u, acc_both, acc_d, a_t, hid_t, d_both, pq_out, hid_out, pq_in, hid_in,
    f_recv, b_recv, r_recv, f_send, b_send, r_send, w_sem, o_sem, out_sem, in_sem,
):
    micro, tokens, d = x.shape
    ff = w_down.shape[0]
    quarters = tokens // Q
    blocks = ff // 128
    me = lax.axis_index("pp")
    stages = 8
    first, last = me == 0, me == stages - 1

    def w_copies():
        for j in range(blocks):
            src = pl.ds(128 * j, 128)
            yield pltpu.make_async_copy(w_gate.at[:, src], w_both.at[:, pl.ds(256 * j, 128)], w_sem.at[0, j])
            yield pltpu.make_async_copy(w_up.at[:, src], w_both.at[:, pl.ds(256 * j + 128, 128)], w_sem.at[1, j])
        yield pltpu.make_async_copy(w_down, w_d, w_sem.at[0, blocks])

    def rows(q, n=Q):
        return pl.ds(pl.multiple_of(q * Q, Q), n)

    def f_copy(m, q, to=None):
        to = jnp.minimum(me + 1, stages - 1) if to is None else to
        return pltpu.make_async_remote_copy(
            f_out.at[m % 2, rows(q)], f_in.at[m, rows(q)], f_send.at[m % 2, q], f_recv.at[m, q], device_id={"pp": to}
        )

    def b_copy(m, q, to=None):
        to = jnp.maximum(me - 1, 0) if to is None else to
        return pltpu.make_async_remote_copy(
            b_out.at[m % 2, rows(q)], b_in.at[m, rows(q)], b_send.at[m % 2, q], b_recv.at[m, q], device_id={"pp": to}
        )

    def f_by_relay(m, q):
        return pltpu.make_async_remote_copy(
            f_out.at[m % 2, rows(q)], r_in.at[m, q // 2], f_send.at[m % 2, q], r_recv.at[m, q // 2], device_id={"pp": RELAY_F}
        )

    def b_by_relay(m, q):
        return pltpu.make_async_remote_copy(
            b_out.at[m % 2, rows(q)], r_in.at[m, q // 2], b_send.at[m % 2, q], r_recv.at[m, q // 2], device_id={"pp": RELAY_B}
        )

    def f_relay(m, q):
        return pltpu.make_async_remote_copy(
            r_in.at[m, q // 2], f_in.at[m, rows(q)], r_send.at[m, q // 2], f_recv.at[m, q], device_id={"pp": 4}
        )

    def b_relay(m, q):
        return pltpu.make_async_remote_copy(
            r_in.at[m, q // 2], b_in.at[m, rows(q)], r_send.at[m, q // 2], b_recv.at[m, q], device_id={"pp": 3}
        )

    def send(m, q, nq, hop, copy, by_relay):
        for k in range(nq):

            @pl.when((me == hop) & ((q + k) % 2 == 0))
            def _():
                by_relay(m, q + k).start()

            @pl.when((me != hop) | ((q + k) % 2 == 1))
            def _():
                copy(m, q + k).start()

    def kept_out(m, q):
        return (
            pltpu.make_async_copy(pq_out.at[rows(q)], kept_pq.at[m, rows(q)], out_sem.at[0, q]),
            pltpu.make_async_copy(hid_out.at[rows(q)], kept_hid.at[m, rows(q)], out_sem.at[1, q]),
        )

    def kept_in(m, q):
        return (
            pltpu.make_async_copy(kept_pq.at[m, rows(q)], pq_in.at[rows(q)], in_sem.at[0, q]),
            pltpu.make_async_copy(kept_hid.at[m, rows(q)], hid_in.at[rows(q)], in_sem.at[1, q]),
        )

    for copy in w_copies():
        copy.start()

    def each(body):
        @pl.loop(0, micro)
        def _(m):
            @pl.loop(0, quarters)
            def _(q):
                body(m, q)

    @pl.when(first)
    def _():
        each(lambda m, q: pltpu.make_async_copy(x.at[m, rows(q)], f_in.at[m, rows(q)], f_recv.at[m, q]).start())

    @pl.when(last)
    def _():
        each(lambda m, q: pltpu.make_async_copy(dy.at[m, rows(q)], b_in.at[m, rows(q)], b_recv.at[m, q]).start())

    barrier = pltpu.get_barrier_semaphore()
    for other in range(1, stages):
        pl.semaphore_signal(barrier, inc=1, device_id={"pp": lax.rem(me + other, stages)})
    acc_both[...] = jnp.zeros_like(acc_both)
    acc_d[...] = jnp.zeros_like(acc_d)
    pl.semaphore_wait(barrier, stages - 1)

    for copy in w_copies():
        copy.wait()

    def scale_of(wide):
        return lax.rsqrt(jnp.mean(wide * wide, -1, keepdims=True) + EPS)

    def gates(both):
        gate, up = both[:, :128], both[:, 128:]
        sig = jax.nn.sigmoid(gate)
        silu = gate * sig
        return silu, up * (sig + silu * (1 - sig)), (silu * up).astype(BF16)

    def forward(m, q, n):
        nq = n // Q
        for k in range(nq):
            f_copy(m, q + k).wait_recv()

        @pl.when(~last)
        def _():
            @pl.when(m >= 1)
            def _():
                for k in range(nq):
                    for copy in kept_out(m - 1, q + k):
                        copy.wait()

            @pl.when(m >= 2)
            def _():
                for k in range(nq):
                    f_copy(m - 2, q + k).wait_send()

            here = rows(q, n)
            h = f_in[m, here]
            wide = h.astype(F32)
            a = (wide * scale_of(wide)).astype(BF16)
            for j in range(blocks):
                silu, by_gate, hid = gates(dot(a, w_both[:, 256 * j : 256 * j + 256]))
                pq_out[here, 256 * j : 256 * j + 128] = silu
                pq_out[here, 256 * j + 128 : 256 * j + 256] = by_gate
                hid_out[here, 128 * j : 128 * j + 128] = hid
            f_out[m % 2, here] = h + dot(hid_out[here], w_d[...]).astype(BF16)
            send(m, q, nq, 3, f_copy, f_by_relay)
            for k in range(nq):
                for copy in kept_out(m, q + k):
                    copy.start()

    def send_back(m, q, n):
        nq = n // Q

        @pl.when(m >= 2)
        def _():
            for k in range(nq):
                b_copy(m - 2, q + k).wait_send()

        here = rows(q, n)
        wide = f_in[m, here].astype(F32)
        scale = scale_of(wide)
        by_a = (dot(d_both[here, :ff], wt_g[...]).astype(BF16) + dot(d_both[here, ff:], wt_u[...]).astype(BF16)).astype(F32)
        by_scale = jnp.sum(by_a * wide, -1, keepdims=True)
        by_wide = by_a * scale - wide * (by_scale * scale * scale * scale * (1.0 / d))
        b_out[m % 2, here] = b_in[m, here] + by_wide.astype(BF16)
        send(m, q, nq, 4, b_copy, b_by_relay)

    def backward_last(m, q, n):
        for k in range(n // Q):
            b_copy(m, q + k).wait_recv()
        here = rows(q, n)
        by_y = b_in[m, here]
        wide = f_in[m, here].astype(F32)
        a = (wide * scale_of(wide)).astype(BF16)
        a_t[:, here] = a.T
        for j in range(0, blocks, 2):
            c = min(2, blocks - j)
            by_hid = dot(by_y, wt_d[:, 128 * j : 128 * (j + c)]).astype(BF16).astype(F32)
            for k in range(j, j + c):
                silu, by_gate, hid = gates(dot(a, w_both[:, 256 * k : 256 * k + 256]))
                by = by_hid[:, 128 * (k - j) : 128 * (k - j) + 128]
                hid_t[128 * k : 128 * k + 128, here] = hid.T
                d_both[here, 128 * k : 128 * k + 128] = (by * by_gate).astype(BF16)
                d_both[here, ff + 128 * k : ff + 128 * k + 128] = (by * silu).astype(BF16)
        send_back(m, q, n)

    def backward(m, q, n):
        nq = n // Q
        for k in range(nq):
            ahead_m, ahead_q = m + (q + k + 2) // quarters, (q + k + 2) % quarters

            @pl.when(ahead_m < micro)
            def _():
                for copy in kept_in(ahead_m, ahead_q):
                    copy.start()

        for k in range(nq):
            for copy in kept_in(m, q + k):
                copy.wait()
            b_copy(m, q + k).wait_recv()
        here = rows(q, n)
        by_y = b_in[m, here]
        wide = f_in[m, here].astype(F32)
        a_t[:, here] = (wide * scale_of(wide)).astype(BF16).T
        hid_t[:, here] = hid_in[here].T
        for j in range(0, blocks, 2):
            c = min(2, blocks - j)
            by_hid = dot(by_y, wt_d[:, 128 * j : 128 * (j + c)]).astype(BF16).astype(F32)
            for k in range(j, j + c):
                by = by_hid[:, 128 * (k - j) : 128 * (k - j) + 128]
                d_both[here, 128 * k : 128 * k + 128] = (by * pq_in[here, 256 * k + 128 : 256 * k + 256]).astype(BF16)
                d_both[here, ff + 128 * k : ff + 128 * k + 128] = (by * pq_in[here, 256 * k : 256 * k + 128]).astype(BF16)

        @pl.when(~first)
        def _():
            send_back(m, q, n)

    def by_weights(m):
        for j in range(blocks):
            cols = slice(256 * j, 256 * j + 256)
            acc_both[:, cols] += dot(a_t[...], d_both[:, cols]).astype(BF16).astype(F32)
        by_y = b_in[m]
        for j in range(0, ff, 352):
            acc_d[j : j + 352, :] += dot(hid_t[j : j + 352, :], by_y).astype(BF16).astype(F32)

    def in_chunks(body, m, fine):
        for n, which in ((FINE, fine), (COARSE, ~fine)):

            @pl.when(which)
            def _():
                @pl.loop(0, tokens // n)
                def _(p):
                    body(m, p * (n // Q), n)

    ahead = jnp.int32(0)
    for s, k in enumerate(AHEAD):
        ahead = jnp.where(me == s, k, ahead)

    @pl.loop(0, micro + max(AHEAD))
    def _(i):
        @pl.when(i < micro)
        def _():
            in_chunks(forward, i, i < FINE_F)

        @pl.when(i == 0)
        def _():
            @pl.loop(0, blocks)
            def _(j):
                cols = pl.ds(pl.multiple_of(128 * j, 128), 128)
                wt_d[:, cols] = w_d[cols, :].T
                wt_g[cols, :] = w_both[:, pl.ds(pl.multiple_of(256 * j, 128), 128)].T
                wt_u[cols, :] = w_both[:, pl.ds(pl.multiple_of(256 * j + 128, 128), 128)].T

        @pl.when((i == micro) & ~last)
        def _():
            for q in range(quarters):
                for copy in kept_out(micro - 1, q):
                    copy.wait()

        @pl.when((i == ahead - 1) & ~last)
        def _():
            for q in range(2):
                for copy in kept_in(0, q):
                    copy.start()

        for device, lag, arrives, relay in ((RELAY_F, LAG_F, f_by_relay, f_relay), (RELAY_B, LAG_B, b_by_relay, b_relay)):

            @pl.when((me == device) & (i >= lag) & (i < micro + lag))
            def _():
                for q in range(0, quarters, 2):
                    arrives(i - lag, q).wait_recv()
                    relay(i - lag, q).start()

        m = i - ahead

        @pl.when((m >= 0) & (m < micro))
        def _():
            fine = (m < FINE_B) | (m >= micro - FINE_E)

            @pl.when(last)
            def _():
                in_chunks(backward_last, m, fine)

            @pl.when(~last)
            def _():
                in_chunks(backward, m, fine)

            by_weights(m)

    for m in range(micro - 2, micro):
        for q in range(quarters):

            @pl.when(~last)
            def _():
                f_copy(m, q).wait_send()

            @pl.when(~first)
            def _():
                b_copy(m, q).wait_send()

    for device, relay in ((RELAY_F, f_relay), (RELAY_B, b_relay)):

        @pl.when(me == device)
        def _():
            @pl.loop(0, micro)
            def _(m):
                for q in range(0, quarters, 2):
                    relay(m, q).wait_send()

    d_both[...] = acc_both[...].astype(BF16)
    hid_t[...] = acc_d[...].astype(BF16)
    out = (
        pltpu.make_async_copy(d_both.at[:, pl.ds(0, ff)], o_gate, o_sem.at[0]),
        pltpu.make_async_copy(d_both.at[:, pl.ds(ff, ff)], o_up, o_sem.at[1]),
        pltpu.make_async_copy(hid_t, o_down, o_sem.at[2]),
    )
    for copy in out:
        copy.start()
    for copy in out:
        copy.wait()


def solution(mesh):
    def step(x, dy, w_gate, w_up, w_down):
        micro, tokens, d = x.shape
        ff = w_down.shape[1]
        quarters = tokens // Q
        hbm = pl.BlockSpec(memory_space=pl.ANY)
        dma = pltpu.SemaphoreType.DMA
        outs = pl.pallas_call(
            kernel,
            out_shape=(
                *(jax.ShapeDtypeStruct(w.shape[1:], w.dtype) for w in (w_gate, w_up, w_down)),
                jax.ShapeDtypeStruct((micro, tokens, 2 * ff), F32),
                jax.ShapeDtypeStruct((micro, tokens, ff), BF16),
            ),
            in_specs=[hbm] * 5,
            out_specs=(hbm,) * 5,
            scratch_shapes=[
                pltpu.VMEM((micro, tokens, d), BF16),
                pltpu.VMEM((micro, tokens, d), BF16),
                pltpu.VMEM((micro, quarters // 2, Q, d), BF16),
                pltpu.VMEM((2, tokens, d), BF16),
                pltpu.VMEM((2, tokens, d), BF16),
                pltpu.VMEM((d, 2 * ff), BF16),
                pltpu.VMEM((ff, d), BF16),
                pltpu.VMEM((d, ff), BF16),
                pltpu.VMEM((ff, d), BF16),
                pltpu.VMEM((ff, d), BF16),
                pltpu.VMEM((d, 2 * ff), F32),
                pltpu.VMEM((ff, d), F32),
                pltpu.VMEM((d, tokens), BF16),
                pltpu.VMEM((ff, tokens), BF16),
                pltpu.VMEM((tokens, 2 * ff), BF16),
                pltpu.VMEM((tokens, 2 * ff), F32),
                pltpu.VMEM((tokens, ff), BF16),
                pltpu.VMEM((tokens, 2 * ff), F32),
                pltpu.VMEM((tokens, ff), BF16),
                dma((micro, quarters)),
                dma((micro, quarters)),
                dma((micro, quarters // 2)),
                dma((2, quarters)),
                dma((2, quarters)),
                dma((micro, quarters // 2)),
                dma((2, ff // 128 + 1)),
                dma((3,)),
                dma((2, quarters)),
                dma((2, quarters)),
            ],
            compiler_params=pltpu.CompilerParams(
                collective_id=0, has_side_effects=True, vmem_limit_bytes=67_043_328
            ),
        )(x, dy, w_gate[0], w_up[0], w_down[0])
        return tuple(o[None] for o in outs[:3])

    return jax.shard_map(
        step,
        mesh=mesh,
        in_specs=(P("rep", None, None),) * 2 + (P("pp", None, None),) * 3,
        out_specs=(P(("rep", "pp"), None, None),) * 3,
        check_vma=False,
    )
```

time: 289 us -> 244 us (0.84)
  Pallas kernels: 283 us -> 238 us
    pallas_call x1, Pallas kernels: 283 us -> 238 us  [step(): pl.pallas_call(kernel, out_shape=(*(jax.ShapeDtypeStruct(w.shape[1:], w.d...]
where the time goes in v3:
time: 244 us
  Pallas kernels  238 us (98%)
  local copies, waits for them, and re-layouts  5.66 us (2%)
    pallas_call x1, Pallas kernels, step(): pl.pallas_call(kernel, out_shape=(*(jax.ShapeDtypeStruct(w.shape[1:], w.d...  238 us
    unnamed x7, local copies, waits for them, and re-layouts  5.66 us

profile of v3, /device:TPU:0, one launch (start us, length us, event | category | flops | bytes accessed | tf_op | source)
XLA Modules:
  0.0 244.1 jit_solution(9296293355212660475)
XLA Ops:
  0.6 237.8 %shard_map.76 = (bf16[512,1408]{1,0:T(8,128)(2,1)}, bf16[512,1408]{1,0:T(8,128)(2,1)}, bf16[1408,512]{1,0:T(8,128)(2,1)}, f32[16,512,2816]{2,1,0:T(8,128)}, bf16[16,512,1408]{2,1,0:T(8,128)(2,1)}) custom-call(bf16[16,512,512]{2,1,0:T(8,128)(2,1)} %x.1, bf16[16,512,512]{2,1,0:T(8,128)(2,1)} %dy.1, bf16[512,1408]{1,0:T(8,128)(2,1)} %bitcast.9, ...), custom_call_target="tpu_custom_call" | custom-call | tf_op jit(solution)/shard_map/pallas_call | solution.py:352
  238.4 0.0 copy-start.1
  238.4 2.7 %copy.11 = bf16[1,512,1408]{2,1,0:T(8,128)(2,1)} copy(bf16[1,512,1408]{2,1,0:T(8,128)(2,1)} %bitcast.8) | data formatting | bytes 2883584
  241.1 0.0 copy-done.1
  241.1 0.0 copy-start
  241.1 1.1 copy.12
  242.2 0.8 copy-done
  243.0 1.1 copy.13
Async XLA Ops:
  238.4 2.7 %copy-start.1 = (bf16[512,1408]{1,0:T(8,128)(2,1)S(1)}, bf16[512,1408]{1,0:T(8,128)(2,1)}, u32[]{:S(2)}) copy-start(bf16[512,1408]{1,0:T(8,128)(2,1)} %get-tuple-element.7) | copy-start | bytes 4325380
  241.1 1.9 copy-start

commit v4 on v3

--- a/solution.py
+++ b/solution.py
@@ -7,15 +7,18 @@
 
 F32, BF16 = jnp.float32, jnp.bfloat16
 EPS = 1e-6
+DOWN = 352
 Q = 128
-COARSE, FINE = 256, 128
-AHEAD = (14, 13, 10, 9, 6, 5, 2, 0)
+COARSE_F, COARSE_B, FINE = 256, 256, 128
+AHEAD = (13, 12, 10, 9, 5, 4, 2, 0)
 FINE_F = 6
-FINE_B = 6
-FINE_E = 6
+FINE_B = 2
+FINE_E = 8
 RELAY_F, RELAY_B = 0, 7
-LAG_F = 3
+LAG_F = 2
 LAG_B = 3
+FROM_F = 3
+UPTO_B = 8
 
 
 def dot(a, b):
@@ -77,14 +80,14 @@
             r_in.at[m, q // 2], b_in.at[m, rows(q)], r_send.at[m, q // 2], b_recv.at[m, q], device_id={"pp": 3}
         )
 
-    def send(m, q, nq, hop, copy, by_relay):
+    def send(m, q, nq, relayed, copy, by_relay):
         for k in range(nq):
 
-            @pl.when((me == hop) & ((q + k) % 2 == 0))
+            @pl.when(relayed & ((q + k) % 2 == 0))
             def _():
                 by_relay(m, q + k).start()
 
-            @pl.when((me != hop) | ((q + k) % 2 == 1))
+            @pl.when(~relayed | ((q + k) % 2 == 1))
             def _():
                 copy(m, q + k).start()
 
@@ -103,21 +106,23 @@
     for copy in w_copies():
         copy.start()
 
-    def each(body):
-        @pl.loop(0, micro)
+    def each(body, start, stop):
+        @pl.loop(start, stop)
         def _(m):
             @pl.loop(0, quarters)
             def _(q):
                 body(m, q)
 
-    @pl.when(first)
-    def _():
-        each(lambda m, q: pltpu.make_async_copy(x.at[m, rows(q)], f_in.at[m, rows(q)], f_recv.at[m, q]).start())
-
-    @pl.when(last)
-    def _():
-        each(lambda m, q: pltpu.make_async_copy(dy.at[m, rows(q)], b_in.at[m, rows(q)], b_recv.at[m, q]).start())
-
+    def load(start, stop):
+        @pl.when(first)
+        def _():
+            each(lambda m, q: pltpu.make_async_copy(x.at[m, rows(q)], f_in.at[m, rows(q)], f_recv.at[m, q]).start(), start, stop)
+
+        @pl.when(last)
+        def _():
+            each(lambda m, q: pltpu.make_async_copy(dy.at[m, rows(q)], b_in.at[m, rows(q)], b_recv.at[m, q]).start(), start, stop)
+
+    load(0, 1)
     barrier = pltpu.get_barrier_semaphore()
     for other in range(1, stages):
         pl.semaphore_signal(barrier, inc=1, device_id={"pp": lax.rem(me + other, stages)})
@@ -127,6 +132,7 @@
 
     for copy in w_copies():
         copy.wait()
+    load(1, micro)
 
     def scale_of(wide):
         return lax.rsqrt(jnp.mean(wide * wide, -1, keepdims=True) + EPS)
@@ -142,33 +148,31 @@
         for k in range(nq):
             f_copy(m, q + k).wait_recv()
 
-        @pl.when(~last)
-        def _():
-            @pl.when(m >= 1)
-            def _():
-                for k in range(nq):
-                    for copy in kept_out(m - 1, q + k):
-                        copy.wait()
-
-            @pl.when(m >= 2)
-            def _():
-                for k in range(nq):
-                    f_copy(m - 2, q + k).wait_send()
-
-            here = rows(q, n)
-            h = f_in[m, here]
-            wide = h.astype(F32)
-            a = (wide * scale_of(wide)).astype(BF16)
-            for j in range(blocks):
-                silu, by_gate, hid = gates(dot(a, w_both[:, 256 * j : 256 * j + 256]))
-                pq_out[here, 256 * j : 256 * j + 128] = silu
-                pq_out[here, 256 * j + 128 : 256 * j + 256] = by_gate
-                hid_out[here, 128 * j : 128 * j + 128] = hid
-            f_out[m % 2, here] = h + dot(hid_out[here], w_d[...]).astype(BF16)
-            send(m, q, nq, 3, f_copy, f_by_relay)
+        @pl.when(m >= 1)
+        def _():
             for k in range(nq):
-                for copy in kept_out(m, q + k):
-                    copy.start()
+                for copy in kept_out(m - 1, q + k):
+                    copy.wait()
+
+        @pl.when(m >= 2)
+        def _():
+            for k in range(nq):
+                f_copy(m - 2, q + k).wait_send()
+
+        here = rows(q, n)
+        h = f_in[m, here]
+        wide = h.astype(F32)
+        a = (wide * scale_of(wide)).astype(BF16)
+        for j in range(blocks):
+            silu, by_gate, hid = gates(dot(a, w_both[:, 256 * j : 256 * j + 256]))
+            pq_out[here, 256 * j : 256 * j + 128] = silu
+            pq_out[here, 256 * j + 128 : 256 * j + 256] = by_gate
+            hid_out[here, 128 * j : 128 * j + 128] = hid
+        f_out[m % 2, here] = h + dot(hid_out[here], w_d[...]).astype(BF16)
+        send(m, q, nq, (me == 3) & (m >= FROM_F), f_copy, f_by_relay)
+        for k in range(nq):
+            for copy in kept_out(m, q + k):
+                copy.start()
 
     def send_back(m, q, n):
         nq = n // Q
@@ -185,11 +189,12 @@
         by_scale = jnp.sum(by_a * wide, -1, keepdims=True)
         by_wide = by_a * scale - wide * (by_scale * scale * scale * scale * (1.0 / d))
         b_out[m % 2, here] = b_in[m, here] + by_wide.astype(BF16)
-        send(m, q, nq, 4, b_copy, b_by_relay)
+        send(m, q, nq, (me == 4) & (m < UPTO_B), b_copy, b_by_relay)
 
     def backward_last(m, q, n):
         for k in range(n // Q):
             b_copy(m, q + k).wait_recv()
+            f_copy(m, q + k).wait_recv()
         here = rows(q, n)
         by_y = b_in[m, here]
         wide = f_in[m, here].astype(F32)
@@ -242,11 +247,38 @@
             cols = slice(256 * j, 256 * j + 256)
             acc_both[:, cols] += dot(a_t[...], d_both[:, cols]).astype(BF16).astype(F32)
         by_y = b_in[m]
-        for j in range(0, ff, 352):
-            acc_d[j : j + 352, :] += dot(hid_t[j : j + 352, :], by_y).astype(BF16).astype(F32)
-
-    def in_chunks(body, m, fine):
-        for n, which in ((FINE, fine), (COARSE, ~fine)):
+        for j in range(0, ff, DOWN):
+            acc_d[j : j + DOWN, :] += dot(hid_t[j : j + DOWN, :], by_y).astype(BF16).astype(F32)
+
+    def out_copies():
+        for j in range(0, ff, DOWN):
+            yield pltpu.make_async_copy(hid_t.at[pl.ds(j, DOWN)], o_down.at[pl.ds(j, DOWN)], o_sem.at[j // DOWN])
+        for j in range(2 * blocks):
+            to = o_gate if j < blocks else o_up
+            yield pltpu.make_async_copy(d_both.at[:, pl.ds(128 * j, 128)], to.at[:, pl.ds(128 * (j % blocks), 128)], o_sem.at[8 + j])
+
+    def last_by_weights(m):
+        by_y = b_in[m]
+        copies = list(out_copies())
+        for j in range(0, ff, DOWN):
+            total = acc_d[j : j + DOWN, :] + dot(hid_t[j : j + DOWN, :], by_y).astype(BF16).astype(F32)
+            hid_t[j : j + DOWN, :] = total.astype(BF16)
+        for copy in copies[: ff // DOWN]:
+            copy.start()
+        for half in range(2):
+            mine = range(half * (blocks // 2), blocks if half else blocks // 2)
+            for j in mine:
+                cols = slice(256 * j, 256 * j + 256)
+                total = acc_both[:, cols] + dot(a_t[...], d_both[:, cols]).astype(BF16).astype(F32)
+                d_both[:, cols] = total.astype(BF16)
+            for j in mine:
+                for copy in copies[ff // DOWN + 2 * j : ff // DOWN + 2 * j + 2]:
+                    copy.start()
+        for copy in copies:
+            copy.wait()
+
+    def in_chunks(body, m, fine, coarse):
+        for n, which in ((FINE, fine), (coarse, ~fine)):
 
             @pl.when(which)
             def _():
@@ -254,24 +286,31 @@
                 def _(p):
                     body(m, p * (n // Q), n)
 
+    def transpose_weights():
+        @pl.loop(0, blocks)
+        def _(j):
+            cols = pl.ds(pl.multiple_of(128 * j, 128), 128)
+            wt_d[:, cols] = w_d[cols, :].T
+            wt_g[cols, :] = w_both[:, pl.ds(pl.multiple_of(256 * j, 128), 128)].T
+            wt_u[cols, :] = w_both[:, pl.ds(pl.multiple_of(256 * j + 128, 128), 128)].T
+
+    @pl.when(~first)
+    def _():
+        transpose_weights()
+
     ahead = jnp.int32(0)
     for s, k in enumerate(AHEAD):
         ahead = jnp.where(me == s, k, ahead)
 
     @pl.loop(0, micro + max(AHEAD))
     def _(i):
-        @pl.when(i < micro)
-        def _():
-            in_chunks(forward, i, i < FINE_F)
-
-        @pl.when(i == 0)
-        def _():
-            @pl.loop(0, blocks)
-            def _(j):
-                cols = pl.ds(pl.multiple_of(128 * j, 128), 128)
-                wt_d[:, cols] = w_d[cols, :].T
-                wt_g[cols, :] = w_both[:, pl.ds(pl.multiple_of(256 * j, 128), 128)].T
-                wt_u[cols, :] = w_both[:, pl.ds(pl.multiple_of(256 * j + 128, 128), 128)].T
+        @pl.when((i < micro) & ~last)
+        def _():
+            in_chunks(forward, i, i < FINE_F, COARSE_F)
+
+        @pl.when((i == 0) & first)
+        def _():
+            transpose_weights()
 
         @pl.when((i == micro) & ~last)
         def _():
@@ -285,9 +324,12 @@
                 for copy in kept_in(0, q):
                     copy.start()
 
-        for device, lag, arrives, relay in ((RELAY_F, LAG_F, f_by_relay, f_relay), (RELAY_B, LAG_B, b_by_relay, b_relay)):
-
-            @pl.when((me == device) & (i >= lag) & (i < micro + lag))
+        for device, lag, arrives, relay, start, stop in (
+            (RELAY_F, LAG_F, f_by_relay, f_relay, FROM_F, micro),
+            (RELAY_B, LAG_B, b_by_relay, b_relay, 0, UPTO_B),
+        ):
+
+            @pl.when((me == device) & (i >= start + lag) & (i < stop + lag))
             def _():
                 for q in range(0, quarters, 2):
                     arrives(i - lag, q).wait_recv()
@@ -301,13 +343,15 @@
 
             @pl.when(last)
             def _():
-                in_chunks(backward_last, m, fine)
+                in_chunks(backward_last, m, fine, COARSE_B)
 
             @pl.when(~last)
             def _():
-                in_chunks(backward, m, fine)
-
-            by_weights(m)
+                in_chunks(backward, m, fine, COARSE_B)
+
+            @pl.when(m < micro - 1)
+            def _():
+                by_weights(m)
 
     for m in range(micro - 2, micro):
         for q in range(quarters):
@@ -320,26 +364,16 @@
             def _():
                 b_copy(m, q).wait_send()
 
-    for device, relay in ((RELAY_F, f_relay), (RELAY_B, b_relay)):
+    for device, relay, start, stop in ((RELAY_F, f_relay, FROM_F, micro), (RELAY_B, b_relay, 0, UPTO_B)):
 
         @pl.when(me == device)
         def _():
-            @pl.loop(0, micro)
+            @pl.loop(start, stop)
             def _(m):
                 for q in range(0, quarters, 2):
                     relay(m, q).wait_send()
 
-    d_both[...] = acc_both[...].astype(BF16)
-    hid_t[...] = acc_d[...].astype(BF16)
-    out = (
-        pltpu.make_async_copy(d_both.at[:, pl.ds(0, ff)], o_gate, o_sem.at[0]),
-        pltpu.make_async_copy(d_both.at[:, pl.ds(ff, ff)], o_up, o_sem.at[1]),
-        pltpu.make_async_copy(hid_t, o_down, o_sem.at[2]),
-    )
-    for copy in out:
-        copy.start()
-    for copy in out:
-        copy.wait()
+    last_by_weights(micro - 1)
 
 
 def solution(mesh):
@@ -385,7 +419,7 @@
                 dma((2, quarters)),
                 dma((micro, quarters // 2)),
                 dma((2, ff // 128 + 1)),
-                dma((3,)),
+                dma((8 + 2 * ff // 128,)),
                 dma((2, quarters)),
                 dma((2, quarters)),
             ],

time: 244 us -> 229 us (0.939)
  Pallas kernels: 238 us -> 222 us
    pallas_call x1, Pallas kernels: 238 us -> 222 us  [step(): pl.pallas_call(kernel, out_shape=(*(jax.ShapeDtypeStruct(w.shape[1:], w.d...]
where the time goes in v4:
time: 229 us
  Pallas kernels  222 us (97%)
  local copies, waits for them, and re-layouts  5.66 us (2%)
    pallas_call x1, Pallas kernels, step(): pl.pallas_call(kernel, out_shape=(*(jax.ShapeDtypeStruct(w.shape[1:], w.d...  222 us
    unnamed x7, local copies, waits for them, and re-layouts  5.66 us

profile of v4, /device:TPU:0, one launch (start us, length us, event | category | flops | bytes accessed | tf_op | source)
XLA Modules:
  0.0 228.7 jit_solution(7832861605024071447)
XLA Ops:
  0.6 222.3 %shard_map.76 = (bf16[512,1408]{1,0:T(8,128)(2,1)}, bf16[512,1408]{1,0:T(8,128)(2,1)}, bf16[1408,512]{1,0:T(8,128)(2,1)}, f32[16,512,2816]{2,1,0:T(8,128)}, bf16[16,512,1408]{2,1,0:T(8,128)(2,1)}) custom-call(bf16[16,512,512]{2,1,0:T(8,128)(2,1)} %x.1, bf16[16,512,512]{2,1,0:T(8,128)(2,1)} %dy.1, bf16[512,1408]{1,0:T(8,128)(2,1)} %bitcast.9, ...), custom_call_target="tpu_custom_call" | custom-call | tf_op jit(solution)/shard_map/pallas_call | solution.py:386
  223.0 0.0 copy-start.1
  223.0 2.7 %copy.11 = bf16[1,512,1408]{2,1,0:T(8,128)(2,1)} copy(bf16[1,512,1408]{2,1,0:T(8,128)(2,1)} %bitcast.8) | data formatting | bytes 2883584
  225.7 0.0 copy-done.1
  225.7 0.0 copy-start
  225.7 1.1 copy.12
  226.8 0.8 copy-done
  227.6 1.1 copy.13
Async XLA Ops:
  223.0 2.7 %copy-start.1 = (bf16[512,1408]{1,0:T(8,128)(2,1)S(1)}, bf16[512,1408]{1,0:T(8,128)(2,1)}, u32[]{:S(2)}) copy-start(bf16[512,1408]{1,0:T(8,128)(2,1)} %get-tuple-element.7) | copy-start | bytes 4325380
  225.7 1.9 copy-start

commit v5 on v4

--- a/solution.py
+++ b/solution.py
@@ -10,10 +10,10 @@
 DOWN = 352
 Q = 128
 COARSE_F, COARSE_B, FINE = 256, 256, 128
-AHEAD = (13, 12, 10, 9, 5, 4, 2, 0)
-FINE_F = 6
+AHEAD = (13, 12, 9, 8, 5, 4, 2, 0)
+FINE_F = 8
 FINE_B = 2
-FINE_E = 8
+FINE_E = 6
 RELAY_F, RELAY_B = 0, 7
 LAG_F = 2
 LAG_B = 3

time: 229 us -> 228 us (level)
  no operation moved by 1% of the time
where the time goes in v5:
time: 228 us
  Pallas kernels  222 us (97%)
  local copies, waits for them, and re-layouts  5.66 us (2%)
    pallas_call x1, Pallas kernels, step(): pl.pallas_call(kernel, out_shape=(*(jax.ShapeDtypeStruct(w.shape[1:], w.d...  222 us
    unnamed x7, local copies, waits for them, and re-layouts  5.66 us

profile of v5, /device:TPU:0, one launch (start us, length us, event | category | flops | bytes accessed | tf_op | source)
XLA Modules:
  0.0 228.1 jit_solution(9749985363575740991)
XLA Ops:
  0.6 221.7 %shard_map.76 = (bf16[512,1408]{1,0:T(8,128)(2,1)}, bf16[512,1408]{1,0:T(8,128)(2,1)}, bf16[1408,512]{1,0:T(8,128)(2,1)}, f32[16,512,2816]{2,1,0:T(8,128)}, bf16[16,512,1408]{2,1,0:T(8,128)(2,1)}) custom-call(bf16[16,512,512]{2,1,0:T(8,128)(2,1)} %x.1, bf16[16,512,512]{2,1,0:T(8,128)(2,1)} %dy.1, bf16[512,1408]{1,0:T(8,128)(2,1)} %bitcast.9, ...), custom_call_target="tpu_custom_call" | custom-call | tf_op jit(solution)/shard_map/pallas_call | solution.py:386
  222.4 0.0 copy-start.1
  222.4 2.7 %copy.11 = bf16[1,512,1408]{2,1,0:T(8,128)(2,1)} copy(bf16[1,512,1408]{2,1,0:T(8,128)(2,1)} %bitcast.8) | data formatting | bytes 2883584
  225.1 0.0 copy-done.1
  225.1 0.0 copy-start
  225.1 1.1 copy.12
  226.2 0.8 copy-done
  227.0 1.1 copy.13
Async XLA Ops:
  222.4 2.7 %copy-start.1 = (bf16[512,1408]{1,0:T(8,128)(2,1)S(1)}, bf16[512,1408]{1,0:T(8,128)(2,1)}, u32[]{:S(2)}) copy-start(bf16[512,1408]{1,0:T(8,128)(2,1)} %get-tuple-element.7) | copy-start | bytes 4325380
  225.1 1.9 copy-start
